TPU v7x, 256 devices: a whole 4x4x8 slice. The times are simulated.
256 devices in a mesh: gx: 32 (over x, z), gy: 8 (over y, core).
Axes of the slice: x: 4, y: 4, z: 8, core: 2. Of those that a mesh axis runs over, the one named last changes fastest.
Arguments:
- velocity_x: float32 [1024, 8, 384], P('gx', 'gy'), may hold values from -6 to 6
- velocity_z: float32 [1024, 8, 384], P('gx', 'gy'), may hold values from -6 to 6
- stress_xx: float32 [1024, 8, 384], P('gx', 'gy'), may hold values from -6 to 6
- stress_zz: float32 [1024, 8, 384], P('gx', 'gy'), may hold values from -6 to 6
- stress_xz: float32 [1024, 8, 384], P('gx', 'gy'), may hold values from -6 to 6
- material: int32 [1024, 8, 384], P('gx', 'gy'), may hold values from 0 to 15, as said below
- land_mask: int32 [1024, 8], P('gx', 'gy'), may hold values 0 or 1
- density: float32 [16], replicated, may hold values from 1 to 3
- lame_lambda: float32 [16], replicated, may hold values from 0.5 to 4
- shear_modulus: float32 [16], replicated, may hold values from 0.3 to 2
- continuation_land: float32 [26, 27], replicated, may hold values from -1.25 to 1.25
- continuation_sea: float32 [26, 27], replicated, may hold values from -1.25 to 1.25
- continuation_bottom: float32 [26, 27], replicated, may hold values from -1.25 to 1.25
Outputs:
- next_velocity_x: float32 [1024, 8, 384], P('gx', 'gy')
- next_velocity_z: float32 [1024, 8, 384], P('gx', 'gy')
- next_stress_xx: float32 [1024, 8, 384], P('gx', 'gy')
- next_stress_zz: float32 [1024, 8, 384], P('gx', 'gy')
- next_stress_xz: float32 [1024, 8, 384], P('gx', 'gy')
Inputs may be any that keep to these rules, and one draw needn't show every extreme that they name: `material`: in every vertical line the layer number never falls with depth, and it is 0 at depth index 0.
All inputs are finite; a program needn't handle non-finite values. No bound on the sum of `land_mask` on one device may be relied on, other than what follows from the above.
Results may differ from a plain program's by a relative error of at most 0.000073.
Values sent between devices are 32-bit elements; how exact they have to be, the bound alone decides.
A program may use at most 64 MiB of HBM per device.

v0:
```python
import functools

import jax
import jax.numpy as jnp
import numpy as np
from jax import lax
from jax.experimental import pallas as pl
from jax.experimental.pallas import tpu as pltpu
from jax.sharding import PartitionSpec as P

NX = 1024
NZ = 384
LAYERS = 16
WINDOW = 27
CONT = 26
RING_X = 4
RING_Z = 8
OWNERS = 32
ROWS = 12
CHUNK = 16
LANES = 128
TILES = 3
TIME_STEP = 0.2


def spectral(length):
    indices = np.arange(length)
    distance = np.mod(indices[:, None] - indices[None, :] + length // 2, length) - length // 2
    parity = 1.0 - 2.0 * np.mod(distance, 2)
    tangent = np.tan(np.pi * np.where(distance == 0, 1, distance) / length)
    return np.where(distance == 0, 0.0, parity * (np.pi / length) / tangent)


def two_parts(matrix):
    high = matrix.astype(np.float32).astype(jnp.bfloat16)
    low = (matrix.astype(np.float32) - high.astype(np.float32)).astype(jnp.bfloat16)
    return high, low


def parts_of(value):
    high = value.astype(jnp.bfloat16)
    low = (value - high.astype(jnp.float32)).astype(jnp.bfloat16)
    return high, low


def dot(left, right):
    return jnp.dot(left, right, preferred_element_type=jnp.float32)


def split_product(left, right_high, right_low):
    rows = left.shape[0]
    high, low = parts_of(left)
    both = dot(jnp.concatenate([high, low], axis=0), right_high)
    return both[:rows] + (both[rows:] + dot(high, right_low))


def swap_blocks(arrays):
    lane = lax.broadcasted_iota(jnp.int32, arrays[0].shape, 1)
    out = list(arrays)
    for bit, width in ((1, 32), (2, 64)):
        upper = (lane & width) != 0
        for k in range(4):
            if k & bit:
                continue
            first, second = out[k], out[k | bit]
            out[k] = jnp.where(upper, pltpu.roll(second, width, 1), first)
            out[k | bit] = jnp.where(upper, second, pltpu.roll(first, LANES - width, 1))
    return out


def lateral(fields, across_high, across_low):
    pairs = []
    for field in fields:
        blocks = field.reshape(4, 2, CHUNK, LANES)
        pairs.append(
            jnp.concatenate(
                [blocks[:, 0].reshape(64, LANES), blocks[:, 1].reshape(64, LANES)], axis=1
            )
        )
    spread = split_product(jnp.concatenate(pairs, axis=0), across_high, across_low)
    results = []
    for f in range(len(fields)):
        pieces = []
        for target in range(4):
            total = None
            for source in range(4):
                shift = (target - source) % 4
                row = 64 * f + CHUNK * source
                term = spread[row : row + CHUNK, 256 * shift : 256 * shift + 256]
                total = term if total is None else total + term
            pieces += [total[:, :LANES], total[:, LANES:]]
        results.append(jnp.concatenate(pieces, axis=0))
    return results


def vertical(lines, land, inner_high, inner_low, edge_high, edge_low):
    lane = lax.broadcasted_iota(jnp.int32, (lines.shape[0], LANES), 1)
    upper = jnp.where(lane < WINDOW, lines[:, :LANES], 0.0)
    lower = jnp.where(lane >= LANES - WINDOW, lines[:, NZ - LANES :], 0.0)
    edges = (
        jnp.where(land, upper, 0.0)
        + pltpu.roll(jnp.where(land, 0.0, upper), 32, 1)
        + pltpu.roll(lower, 64 + WINDOW, 1)
    )
    return split_product(lines, inner_high, inner_low) + split_product(edges, edge_high, edge_low)


def load_lines(ref):
    return jnp.concatenate([ref[pl.ds(t, 32, stride=TILES), :] for t in range(TILES)], axis=1)


def store_lines(ref, value):
    for t in range(TILES):
        ref[pl.ds(t, 32, stride=TILES), :] = value[:, LANES * t : LANES * (t + 1)]


def kernel(
    vx_hbm, vz_hbm, xx_hbm, zz_hbm, xz_hbm, material_hbm,
    land_ref, density_ref, lame_ref, shear_ref, gland_ref, gsea_ref, gbottom_ref, bound_ref,
    inner_high_hbm, inner_low_hbm, across_high_hbm, across_low_hbm,
    vx_out, vz_out, xx_out, zz_out, xz_out,
    vx_ref, vz_ref, xx_ref, zz_ref, xz_ref, material_ref,
    inner_high_ref, inner_low_ref, across_high_ref, across_low_ref,
    packed, outgoing, incoming, returned, home, load_sem,
    send_sem, recv_sem, send_back_sem, recv_back_sem,
):
    me = lax.axis_index("gx")
    my_x, my_z = me // RING_Z, me % RING_Z

    def offset(step):
        group = step // 4
        half = (group + 1) // 2
        dz = 4 + half * (1 - 2 * (group % 2))
        dx = (2 + (step % 4)) % 4
        return dx, dz

    def ahead(step):
        dx, dz = offset(step)
        return ((my_x + dx) % RING_X) * RING_Z + (my_z + dz) % RING_Z

    def behind(step):
        dx, dz = offset(step)
        return ((my_x + RING_X - dx) % RING_X) * RING_Z + (my_z + 2 * RING_Z - dz) % RING_Z

    def is_other(step):
        dx, dz = offset(step)
        return dx + (dz % RING_Z) != 0

    barrier = pltpu.get_barrier_semaphore()

    def greet(step, carry):
        @pl.when(is_other(step))
        def _():
            pl.semaphore_signal(barrier, inc=1, device_id={"gx": ahead(step)})

        return carry

    lax.fori_loop(0, OWNERS, greet, 0)

    pairs = (
        (material_hbm, material_ref), (xz_hbm, xz_ref), (zz_hbm, zz_ref),
        (inner_high_hbm, inner_high_ref), (inner_low_hbm, inner_low_ref),
        (vx_hbm, vx_ref), (vz_hbm, vz_ref), (xx_hbm, xx_ref),
        (across_high_hbm, across_high_ref), (across_low_hbm, across_low_ref),
    )
    loads = [pltpu.make_async_copy(a, b, load_sem.at[i]) for i, (a, b) in enumerate(pairs)]
    for load in loads:
        load.start()

    diagonal = lax.broadcasted_iota(jnp.int32, (32, 32), 0) == lax.broadcasted_iota(
        jnp.int32, (32, 32), 1
    )
    land = (
        jnp.sum(
            jnp.where(diagonal, jnp.broadcast_to(land_ref[...], (32, 32)), 0),
            axis=1,
            keepdims=True,
        )
        > 0
    )
    land_pair = jnp.broadcast_to(jnp.concatenate([land, land], axis=0), (64, LANES))

    gap = jnp.zeros((CONT, 32 - WINDOW), jnp.float32)
    grams = jnp.concatenate(
        [gland_ref[...], gap, gsea_ref[...], gap, gbottom_ref[...], gap,
         jnp.zeros((CONT, 32), jnp.float32)],
        axis=1,
    )
    folded = lax.dot_general(
        grams, bound_ref[...], (((0,), (0,)), ((), ())),
        precision=lax.Precision.HIGHEST, preferred_element_type=jnp.float32,
    )
    edge_high, edge_low = parts_of(folded)

    loads[0].wait()
    material = load_lines(material_ref)
    density = jnp.full(material.shape, density_ref[0], jnp.float32)
    lame = jnp.full(material.shape, lame_ref[0], jnp.float32)
    shear = jnp.full(material.shape, shear_ref[0], jnp.float32)
    for layer in range(1, LAYERS):
        chosen = material == layer
        density = jnp.where(chosen, density_ref[layer], density)
        lame = jnp.where(chosen, lame_ref[layer], lame)
        shear = jnp.where(chosen, shear_ref[layer], shear)
    light = TIME_STEP * (1.0 / density)

    for load in loads[1:5]:
        load.wait()
    inner_high, inner_low = inner_high_ref[...], inner_low_ref[...]
    stress_xz = load_lines(xz_ref)
    stress_zz = load_lines(zz_ref)
    depth = vertical(
        jnp.concatenate([stress_xz, stress_zz], axis=0), land_pair,
        inner_high, inner_low, edge_high, edge_low,
    )
    for load in loads[5:8]:
        load.wait()
    stress_xx = load_lines(xx_ref)
    part_vx = load_lines(vx_ref) + light * depth[:32]
    part_vz = load_lines(vz_ref) + light * depth[32:]

    packed[0] = jnp.concatenate([stress_xx, stress_xz, part_vx, part_vz], axis=0).T
    packed[1] = jnp.concatenate(
        [light] + [pltpu.roll(light, NZ - 3 * slot, 1) for slot in range(1, 4)], axis=0
    ).T
    for owner in range(OWNERS):
        outgoing[owner, :ROWS] = packed[0, ROWS * owner : ROWS * (owner + 1)]
        outgoing[owner, ROWS:] = packed[1, ROWS * owner : ROWS * owner + CHUNK - ROWS]
    incoming[me] = outgoing[me]

    pl.semaphore_wait(barrier, OWNERS - 1)

    def out_copy(step):
        return pltpu.make_async_remote_copy(
            src_ref=outgoing.at[ahead(step)], dst_ref=incoming.at[me],
            send_sem=send_sem.at[step], recv_sem=recv_sem.at[step],
            device_id={"gx": ahead(step)},
        )

    def in_copy(step):
        return pltpu.make_async_remote_copy(
            src_ref=outgoing.at[ahead(step)], dst_ref=incoming.at[behind(step)],
            send_sem=send_sem.at[step], recv_sem=recv_sem.at[step],
            device_id={"gx": ahead(step)},
        )

    def back_copy(step):
        return pltpu.make_async_remote_copy(
            src_ref=returned.at[ahead(step)], dst_ref=home.at[me],
            send_sem=send_back_sem.at[step], recv_sem=recv_back_sem.at[step],
            device_id={"gx": ahead(step)},
        )

    def home_copy(step):
        return pltpu.make_async_remote_copy(
            src_ref=returned.at[ahead(step)], dst_ref=home.at[behind(step)],
            send_sem=send_back_sem.at[step], recv_sem=recv_back_sem.at[step],
            device_id={"gx": ahead(step)},
        )

    def each_other(act):
        def step_of(step, carry):
            @pl.when(is_other(step))
            def _():
                act(step)

            return carry

        lax.fori_loop(0, OWNERS, step_of, 0)

    each_other(lambda step: out_copy(step).start())
    each_other(lambda step: in_copy(step).wait_recv())
    for load in loads[8:]:
        load.wait()
    across_high, across_low = across_high_ref[...], across_low_ref[...]

    got = incoming[...].reshape(8, 4, CHUNK, LANES)
    fields = swap_blocks([got[:, k].reshape(8 * CHUNK, LANES) for k in range(4)])
    row = lax.broadcasted_iota(jnp.int32, (8 * CHUNK, LANES), 0) % CHUNK
    factor = jnp.zeros((8 * CHUNK, LANES), jnp.float32)
    for slot in range(4):
        moved = pltpu.roll(fields[slot], 8 * CHUNK + 3 * slot - ROWS, 0)
        factor = jnp.where((row >= 3 * slot) & (row < 3 * slot + 3), moved, factor)
    slope = lateral(fields[:2], across_high, across_low)
    moved_vx = fields[2] + factor * slope[0]
    moved_vz = fields[3] + factor * slope[1]
    slope = lateral([moved_vx, moved_vz], across_high, across_low)
    back = swap_blocks([moved_vx, moved_vz, slope[0], slope[1]])
    for k in range(4):
        for group in range(8):
            returned[4 * group + k] = back[k][CHUNK * group : CHUNK * group + ROWS]
    home[me] = returned[me]

    each_other(lambda step: back_copy(step).start())
    each_other(lambda step: home_copy(step).wait_recv())

    for owner in range(OWNERS):
        packed[0, ROWS * owner : ROWS * (owner + 1)] = home[owner]
    settled = packed[0].T
    next_vx, next_vz = settled[:32], settled[32:64]
    lateral_vx, lateral_vz = settled[64:96], settled[96:]
    depth = vertical(
        settled[:64], land_pair, inner_high_ref[...], inner_low_ref[...], edge_high, edge_low
    )
    depth_vx, depth_vz = depth[:32], depth[32:]
    normal = lame + 2.0 * shear
    surface = lax.broadcasted_iota(jnp.int32, (32, NZ), 1) == 0
    next_xx = load_lines(xx_ref) + TIME_STEP * (normal * lateral_vx + lame * depth_vz)
    next_zz = load_lines(zz_ref) + TIME_STEP * (lame * lateral_vx + normal * depth_vz)
    next_xz = load_lines(xz_ref) + TIME_STEP * shear * (depth_vx + lateral_vz)
    next_zz = jnp.where(surface & jnp.broadcast_to(land, (32, NZ)), 0.0, next_zz)
    next_xz = jnp.where(surface, 0.0, next_xz)
    store_lines(vx_out, next_vx)
    store_lines(vz_out, next_vz)
    store_lines(xx_out, next_xx)
    store_lines(zz_out, next_zz)
    store_lines(xz_out, next_xz)

    each_other(lambda step: in_copy(step).wait_send())
    each_other(lambda step: home_copy(step).wait_send())


def body(
    velocity_x, velocity_z, stress_xx, stress_zz, stress_xz, material, land_mask,
    density, lame_lambda, shear_modulus, continuation_land, continuation_sea, continuation_bottom,
):
    across = spectral(NX)
    depth = spectral(NZ + CONT)
    across_high, across_low = two_parts(across[:, :256].T)
    inner_high, inner_low = two_parts(depth[:NZ, :NZ].T)
    bound = depth[:NZ, NZ:].T.astype(np.float32)

    flat = [
        a.reshape(32 * TILES, LANES)
        for a in (velocity_x, velocity_z, stress_xx, stress_zz, stress_xz, material)
    ]
    vmem = pl.BlockSpec(memory_space=pltpu.VMEM)
    smem = pl.BlockSpec(memory_space=pltpu.SMEM)
    hbm = pl.BlockSpec(memory_space=pltpu.HBM)
    lines = pltpu.VMEM((32 * TILES, LANES), jnp.float32)
    outs = pl.pallas_call(
        kernel,
        out_shape=[jax.ShapeDtypeStruct((32 * TILES, LANES), jnp.float32)] * 5,
        in_specs=[hbm] * 6 + [vmem] + [smem] * 3 + [vmem] * 4 + [hbm] * 4,
        out_specs=[vmem] * 5,
        scratch_shapes=[lines] * 5 + [
            pltpu.VMEM((32 * TILES, LANES), jnp.int32),
            pltpu.VMEM((NZ, NZ), jnp.bfloat16),
            pltpu.VMEM((NZ, NZ), jnp.bfloat16),
            pltpu.VMEM((256, NX), jnp.bfloat16),
            pltpu.VMEM((256, NX), jnp.bfloat16),
            pltpu.VMEM((2, NZ, LANES), jnp.float32),
            pltpu.VMEM((OWNERS, CHUNK, LANES), jnp.float32),
            pltpu.VMEM((OWNERS, CHUNK, LANES), jnp.float32),
            pltpu.VMEM((OWNERS, ROWS, LANES), jnp.float32),
            pltpu.VMEM((OWNERS, ROWS, LANES), jnp.float32),
            pltpu.SemaphoreType.DMA((10,)),
            pltpu.SemaphoreType.DMA((OWNERS,)),
            pltpu.SemaphoreType.DMA((OWNERS,)),
            pltpu.SemaphoreType.DMA((OWNERS,)),
            pltpu.SemaphoreType.DMA((OWNERS,)),
        ],
        compiler_params=pltpu.CompilerParams(collective_id=0, has_side_effects=True),
    )(
        *flat, land_mask.reshape(1, 32), density, lame_lambda, shear_modulus,
        continuation_land, continuation_sea, continuation_bottom, jnp.asarray(bound),
        jnp.asarray(inner_high), jnp.asarray(inner_low),
        jnp.asarray(across_high), jnp.asarray(across_low),
    )
    return tuple(a.reshape(32, 1, NZ) for a in outs)


def solution(mesh):
    split = P("gx", "gy", None)
    return jax.shard_map(
        body,
        mesh=mesh,
        in_specs=(split,) * 6 + (P("gx", "gy"),) + (P(),) * 6,
        out_specs=(split,) * 5,
        check_vma=False,
    )
```

profile of v0, /device:TPU:8, one launch (start us, length us, event | category | flops | bytes accessed | tf_op | source)
XLA Modules:
  0.0 36.6 jit_solution(5194709020966160914)
XLA Ops:
  0.6 31.4 %shard_map.209 = (f32[96,128]{1,0:T(8,128)}, f32[96,128]{1,0:T(8,128)}, f32[96,128]{1,0:T(8,128)}, f32[96,128]{1,0:T(8,128)}, f32[96,128]{1,0:T(8,128)}) custom-call(f32[96,128]{1,0:T(8,128)} %bitcast.17, f32[96,128]{1,0:T(8,128)} %bitcast.18, f32[96,128]{1,0:T(8,128)} %bitcast.19, f32[96,128]{1,0:T(8,128)} %bitcast.20, f32[96,128]{1,0:T(8,128)} %bitcast.21, ...), custom_call_target="tpu_custom_call" | custom-call | tf_op jit(solution)/shard_map/pallas_call | solution.py:341
  32.1 0.0 copy-start.3
  32.1 1.5 %copy.33 = f32[32,1,384]{2,1,0:T(1,128)} copy(f32[32,1,384]{2,1,0:T(1,128)} %bitcast.16) | data formatting | bytes 98304
  33.6 0.0 copy-done.3
  33.6 0.0 copy-start.2
  33.6 0.6 %copy.34 = f32[32,1,384]{2,1,0:T(1,128)} copy(f32[32,1,384]{2,1,0:T(1,128)S(1)} %bitcast.15) | data formatting | bytes 98304
  34.2 0.2 copy-done.2
  34.4 0.0 copy-start.1
  34.4 0.6 %copy.35 = f32[32,1,384]{2,1,0:T(1,128)} copy(f32[32,1,384]{2,1,0:T(1,128)S(1)} %bitcast.14) | data formatting | bytes 98304
  35.0 0.2 copy-done.1
  35.2 0.0 copy-start
  35.2 0.6 %copy.36 = f32[32,1,384]{2,1,0:T(1,128)} copy(f32[32,1,384]{2,1,0:T(1,128)S(1)} %bitcast.13) | data formatting | bytes 98304
  35.8 0.2 copy-done
  36.0 0.6 %copy.37 = f32[32,1,384]{2,1,0:T(1,128)} copy(f32[32,1,384]{2,1,0:T(1,128)S(1)} %bitcast.12) | data formatting | bytes 98304
Async XLA Ops:
  32.1 1.5 %copy-start.3 = (f32[96,128]{1,0:T(8,128)S(1)}, f32[96,128]{1,0:T(8,128)}, u32[]{:S(2)}) copy-start(f32[96,128]{1,0:T(8,128)} %get-tuple-element.11) | copy-start | bytes 147460
  33.6 0.8 %copy-start.2 = (f32[96,128]{1,0:T(8,128)S(1)}, f32[96,128]{1,0:T(8,128)}, u32[]{:S(2)}) copy-start(f32[96,128]{1,0:T(8,128)} %get-tuple-element.12) | copy-start | bytes 147460
  34.4 0.8 %copy-start.1 = (f32[96,128]{1,0:T(8,128)S(1)}, f32[96,128]{1,0:T(8,128)}, u32[]{:S(2)}) copy-start(f32[96,128]{1,0:T(8,128)} %get-tuple-element.13) | copy-start | bytes 147460
  35.2 0.8 %copy-start = (f32[96,128]{1,0:T(8,128)S(1)}, f32[96,128]{1,0:T(8,128)}, u32[]{:S(2)}) copy-start(f32[96,128]{1,0:T(8,128)} %get-tuple-element.14) | copy-start | bytes 147460
where the time goes:
time: 37 us; the launch traced here: 36.6 us
  Pallas kernels  31.4 us (85%)
  local copies, waits for them, and re-layouts  4.52 us (12%)
  between operations  0.66 us (2%)
    pallas_call x1, Pallas kernels, body(): pl.pallas_call(kernel, out_shape=[jax.ShapeDtypeStruct((32 * TILES, LANES...  31.4 us
    unnamed x13, local copies, waits for them, and re-layouts  4.52 us

commit v1 on v0

--- a/solution.py
+++ b/solution.py
@@ -21,6 +21,7 @@
 LANES = 128
 TILES = 3
 TIME_STEP = 0.2
+VMEM_KIB = 63900
 
 
 def spectral(length):
@@ -116,12 +117,13 @@
 
 def kernel(
     vx_hbm, vz_hbm, xx_hbm, zz_hbm, xz_hbm, material_hbm,
-    land_ref, density_ref, lame_ref, shear_ref, gland_ref, gsea_ref, gbottom_ref, bound_ref,
+    land_hbm, density_hbm, lame_hbm, shear_hbm, gland_hbm, gsea_hbm, gbottom_hbm, bound_hbm,
     inner_high_hbm, inner_low_hbm, across_high_hbm, across_low_hbm,
-    vx_out, vz_out, xx_out, zz_out, xz_out,
-    vx_ref, vz_ref, xx_ref, zz_ref, xz_ref, material_ref,
-    inner_high_ref, inner_low_ref, across_high_ref, across_low_ref,
-    packed, outgoing, incoming, returned, home, load_sem,
+    home, coefs, side, edge_high_out, edge_low_out, inner_high_ref, inner_low_ref,
+    xx_ref, zz_ref, xz_ref,
+    vx_ref, vz_ref, material_ref, land_ref, density_ref, lame_ref, shear_ref,
+    gland_ref, gsea_ref, gbottom_ref, bound_ref, across_high_ref, across_low_ref,
+    packed, outgoing, incoming, returned, load_sem,
     send_sem, recv_sem, send_back_sem, recv_back_sem,
 ):
     me = lax.axis_index("gx")
@@ -158,6 +160,9 @@
     lax.fori_loop(0, OWNERS, greet, 0)
 
     pairs = (
+        (land_hbm, land_ref), (gland_hbm, gland_ref), (gsea_hbm, gsea_ref),
+        (gbottom_hbm, gbottom_ref), (bound_hbm, bound_ref),
+        (density_hbm, density_ref), (lame_hbm, lame_ref), (shear_hbm, shear_ref),
         (material_hbm, material_ref), (xz_hbm, xz_ref), (zz_hbm, zz_ref),
         (inner_high_hbm, inner_high_ref), (inner_low_hbm, inner_low_ref),
         (vx_hbm, vx_ref), (vz_hbm, vz_ref), (xx_hbm, xx_ref),
@@ -166,6 +171,8 @@
     loads = [pltpu.make_async_copy(a, b, load_sem.at[i]) for i, (a, b) in enumerate(pairs)]
     for load in loads:
         load.start()
+    for load in loads[:5]:
+        load.wait()
 
     diagonal = lax.broadcasted_iota(jnp.int32, (32, 32), 0) == lax.broadcasted_iota(
         jnp.int32, (32, 32), 1
@@ -179,6 +186,7 @@
         > 0
     )
     land_pair = jnp.broadcast_to(jnp.concatenate([land, land], axis=0), (64, LANES))
+    side[...] = land_pair.astype(jnp.int32)
 
     gap = jnp.zeros((CONT, 32 - WINDOW), jnp.float32)
     grams = jnp.concatenate(
@@ -191,8 +199,11 @@
         precision=lax.Precision.HIGHEST, preferred_element_type=jnp.float32,
     )
     edge_high, edge_low = parts_of(folded)
-
-    loads[0].wait()
+    edge_high_out[...] = edge_high
+    edge_low_out[...] = edge_low
+
+    for load in loads[5:9]:
+        load.wait()
     material = load_lines(material_ref)
     density = jnp.full(material.shape, density_ref[0], jnp.float32)
     lame = jnp.full(material.shape, lame_ref[0], jnp.float32)
@@ -203,8 +214,10 @@
         lame = jnp.where(chosen, lame_ref[layer], lame)
         shear = jnp.where(chosen, shear_ref[layer], shear)
     light = TIME_STEP * (1.0 / density)
-
-    for load in loads[1:5]:
+    coefs[0] = lame
+    coefs[1] = shear
+
+    for load in loads[9:13]:
         load.wait()
     inner_high, inner_low = inner_high_ref[...], inner_low_ref[...]
     stress_xz = load_lines(xz_ref)
@@ -213,7 +226,7 @@
         jnp.concatenate([stress_xz, stress_zz], axis=0), land_pair,
         inner_high, inner_low, edge_high, edge_low,
     )
-    for load in loads[5:8]:
+    for load in loads[13:16]:
         load.wait()
     stress_xx = load_lines(xx_ref)
     part_vx = load_lines(vx_ref) + light * depth[:32]
@@ -270,7 +283,7 @@
 
     each_other(lambda step: out_copy(step).start())
     each_other(lambda step: in_copy(step).wait_recv())
-    for load in loads[8:]:
+    for load in loads[16:]:
         load.wait()
     across_high, across_low = across_high_ref[...], across_low_ref[...]
 
@@ -294,30 +307,41 @@
     each_other(lambda step: back_copy(step).start())
     each_other(lambda step: home_copy(step).wait_recv())
 
+    each_other(lambda step: in_copy(step).wait_send())
+    each_other(lambda step: home_copy(step).wait_send())
+
+
+def last_kernel(
+    home, coefs, side, edge_high_ref, edge_low_ref, inner_high_ref, inner_low_ref,
+    xx_ref, zz_ref, xz_ref,
+    vx_out, vz_out, xx_out, zz_out, xz_out,
+    packed,
+):
     for owner in range(OWNERS):
-        packed[0, ROWS * owner : ROWS * (owner + 1)] = home[owner]
-    settled = packed[0].T
+        packed[ROWS * owner : ROWS * (owner + 1)] = home[owner]
+    settled = packed[...].T
     next_vx, next_vz = settled[:32], settled[32:64]
+    store_lines(vx_out, next_vx)
+    store_lines(vz_out, next_vz)
     lateral_vx, lateral_vz = settled[64:96], settled[96:]
+    land = side[...] > 0
     depth = vertical(
-        settled[:64], land_pair, inner_high_ref[...], inner_low_ref[...], edge_high, edge_low
+        settled[:64], land, inner_high_ref[...], inner_low_ref[...],
+        edge_high_ref[...], edge_low_ref[...],
     )
     depth_vx, depth_vz = depth[:32], depth[32:]
+    lame, shear = coefs[0], coefs[1]
     normal = lame + 2.0 * shear
     surface = lax.broadcasted_iota(jnp.int32, (32, NZ), 1) == 0
     next_xx = load_lines(xx_ref) + TIME_STEP * (normal * lateral_vx + lame * depth_vz)
     next_zz = load_lines(zz_ref) + TIME_STEP * (lame * lateral_vx + normal * depth_vz)
     next_xz = load_lines(xz_ref) + TIME_STEP * shear * (depth_vx + lateral_vz)
-    next_zz = jnp.where(surface & jnp.broadcast_to(land, (32, NZ)), 0.0, next_zz)
+    on_land = jnp.concatenate([land[:32]] * TILES, axis=1)
+    next_zz = jnp.where(surface & on_land, 0.0, next_zz)
     next_xz = jnp.where(surface, 0.0, next_xz)
-    store_lines(vx_out, next_vx)
-    store_lines(vz_out, next_vz)
     store_lines(xx_out, next_xx)
     store_lines(zz_out, next_zz)
     store_lines(xz_out, next_xz)
-
-    each_other(lambda step: in_copy(step).wait_send())
-    each_other(lambda step: home_copy(step).wait_send())
 
 
 def body(
@@ -335,38 +359,57 @@
         for a in (velocity_x, velocity_z, stress_xx, stress_zz, stress_xz, material)
     ]
     vmem = pl.BlockSpec(memory_space=pltpu.VMEM)
-    smem = pl.BlockSpec(memory_space=pltpu.SMEM)
     hbm = pl.BlockSpec(memory_space=pltpu.HBM)
     lines = pltpu.VMEM((32 * TILES, LANES), jnp.float32)
-    outs = pl.pallas_call(
+    square = pltpu.VMEM((NZ, NZ), jnp.bfloat16)
+    edge = pltpu.VMEM((LANES, NZ), jnp.bfloat16)
+    gram = pltpu.VMEM((CONT, WINDOW), jnp.float32)
+    layers = pltpu.SMEM((LAYERS,), jnp.float32)
+    kept = pl.pallas_call(
         kernel,
-        out_shape=[jax.ShapeDtypeStruct((32 * TILES, LANES), jnp.float32)] * 5,
-        in_specs=[hbm] * 6 + [vmem] + [smem] * 3 + [vmem] * 4 + [hbm] * 4,
-        out_specs=[vmem] * 5,
-        scratch_shapes=[lines] * 5 + [
+        out_shape=[
+            pltpu.VMEM((OWNERS, ROWS, LANES), jnp.float32),
+            pltpu.VMEM((2, 32, NZ), jnp.float32),
+            pltpu.VMEM((64, LANES), jnp.int32),
+            edge, edge, square, square, lines, lines, lines,
+        ],
+        in_specs=[hbm] * 18,
+        out_specs=[vmem] * 10,
+        scratch_shapes=[
+            lines, lines,
             pltpu.VMEM((32 * TILES, LANES), jnp.int32),
-            pltpu.VMEM((NZ, NZ), jnp.bfloat16),
-            pltpu.VMEM((NZ, NZ), jnp.bfloat16),
+            pltpu.VMEM((1, 32), jnp.int32),
+            layers, layers, layers, gram, gram, gram,
+            pltpu.VMEM((CONT, NZ), jnp.float32),
             pltpu.VMEM((256, NX), jnp.bfloat16),
             pltpu.VMEM((256, NX), jnp.bfloat16),
             pltpu.VMEM((2, NZ, LANES), jnp.float32),
             pltpu.VMEM((OWNERS, CHUNK, LANES), jnp.float32),
             pltpu.VMEM((OWNERS, CHUNK, LANES), jnp.float32),
             pltpu.VMEM((OWNERS, ROWS, LANES), jnp.float32),
-            pltpu.VMEM((OWNERS, ROWS, LANES), jnp.float32),
-            pltpu.SemaphoreType.DMA((10,)),
+            pltpu.SemaphoreType.DMA((18,)),
             pltpu.SemaphoreType.DMA((OWNERS,)),
             pltpu.SemaphoreType.DMA((OWNERS,)),
             pltpu.SemaphoreType.DMA((OWNERS,)),
             pltpu.SemaphoreType.DMA((OWNERS,)),
         ],
-        compiler_params=pltpu.CompilerParams(collective_id=0, has_side_effects=True),
+        compiler_params=pltpu.CompilerParams(
+            collective_id=0, has_side_effects=True, vmem_limit_bytes=VMEM_KIB * 1024
+        ),
     )(
         *flat, land_mask.reshape(1, 32), density, lame_lambda, shear_modulus,
         continuation_land, continuation_sea, continuation_bottom, jnp.asarray(bound),
         jnp.asarray(inner_high), jnp.asarray(inner_low),
         jnp.asarray(across_high), jnp.asarray(across_low),
     )
+    outs = pl.pallas_call(
+        last_kernel,
+        out_shape=[jax.ShapeDtypeStruct((32 * TILES, LANES), jnp.float32)] * 5,
+        in_specs=[vmem] * 10,
+        out_specs=[vmem] * 5,
+        scratch_shapes=[pltpu.VMEM((NZ, LANES), jnp.float32)],
+        compiler_params=pltpu.CompilerParams(vmem_limit_bytes=8 * 2**20),
+    )(*kept)
     return tuple(a.reshape(32, 1, NZ) for a in outs)
 
 

time: 37 us -> 31.2 us (0.84)
  local copies, waits for them, and re-layouts: 4.52 us -> 0 us
  Pallas kernels: 31.4 us -> 30.4 us
    unnamed x13 -> x0, local copies, waits for them, and re-layouts: 4.52 us -> none
    pallas_call x1 -> x2, Pallas kernels: 31.4 us -> 30.4 us  [the longest x1 29.4 us: body(): pl.pallas_call(kernel, out_shape=[pltpu.VMEM((OWNERS, ROWS, LANES), jnp.f...]
where the time goes in v1:
time: 31.2 us; the launch traced here: 31.1 us
  Pallas kernels  30.4 us (97%)
  between operations  0.64 us (2%)
    pallas_call x1, Pallas kernels, body(): pl.pallas_call(kernel, out_shape=[pltpu.VMEM((OWNERS, ROWS, LANES), jnp.f...  29.4 us
    pallas_call x1, Pallas kernels, body(): pl.pallas_call(last_kernel, out_shape=[jax.ShapeDtypeStruct((32 * TILES,...  1.06 us

profile of v1, /device:TPU:8, one launch (start us, length us, event | category | flops | bytes accessed | tf_op | source)
XLA Modules:
  0.0 31.1 jit_solution(5160040000081324712)
XLA Ops:
  0.6 29.4 %shard_map.209 = (f32[32,12,128]{2,1,0:T(8,128)S(1)}, f32[2,32,384]{2,1,0:T(8,128)S(1)}, s32[64,128]{1,0:T(8,128)S(1)}, bf16[128,384]{1,0:T(8,128)(2,1)S(1)}, bf...) custom-call(f32[96,128]{1,0:T(8,128)} %bitcast.12, ...), custom_call_target="tpu_custom_call" | custom-call | tf_op jit(solution)/shard_map/pallas_call | solution.py:368
  30.0 1.1 %shard_map.210 = (f32[96,128]{1,0:T(8,128)}, f32[96,128]{1,0:T(8,128)}, f32[96,128]{1,0:T(8,128)}, f32[96,128]{1,0:T(8,128)}, f32[96,128]{1,0:T(8,128)}) custom-call(f32[32,12,128]{2,1,0:T(8,128)S(1)} %get-tuple-element.20.home, f32[2,32,384]{2,1,0:T(8,128)S(1)} %get-tuple-element.21.coefs, s32[64,128]{1,0:T(8,128)S(1)} %get-tuple-element.22.side, ...), custom_call_target="tpu_custom_call" | custom-call | tf_op jit(solution)/shard_map/pallas_call | solution.py:405

commit v2 on v1

--- a/solution.py
+++ b/solution.py
@@ -24,6 +24,16 @@
 VMEM_KIB = 63900
 
 
+ORDER = [
+    (dx, sign * dz % RING_Z)
+    for dz in (4, 3, 2, 1, 0)
+    for dx in (2, 1, 3, 0)
+    for sign in ((1, -1) if dz % 4 else (1,))
+    if dx or dz
+]
+PIECES = (4, 8)
+
+
 def spectral(length):
     indices = np.arange(length)
     distance = np.mod(indices[:, None] - indices[None, :] + length // 2, length) - length // 2
@@ -70,12 +80,13 @@
 
 
 def lateral(fields, across_high, across_low):
+    height = fields[0].shape[0] // 8
     pairs = []
     for field in fields:
-        blocks = field.reshape(4, 2, CHUNK, LANES)
+        blocks = field.reshape(4, 2, height, LANES)
         pairs.append(
             jnp.concatenate(
-                [blocks[:, 0].reshape(64, LANES), blocks[:, 1].reshape(64, LANES)], axis=1
+                [blocks[:, half].reshape(4 * height, LANES) for half in range(2)], axis=1
             )
         )
     spread = split_product(jnp.concatenate(pairs, axis=0), across_high, across_low)
@@ -86,8 +97,8 @@
             total = None
             for source in range(4):
                 shift = (target - source) % 4
-                row = 64 * f + CHUNK * source
-                term = spread[row : row + CHUNK, 256 * shift : 256 * shift + 256]
+                row = height * (4 * f + source)
+                term = spread[row : row + height, 256 * shift : 256 * shift + 256]
                 total = term if total is None else total + term
             pieces += [total[:, :LANES], total[:, LANES:]]
         results.append(jnp.concatenate(pieces, axis=0))
@@ -119,45 +130,28 @@
     vx_hbm, vz_hbm, xx_hbm, zz_hbm, xz_hbm, material_hbm,
     land_hbm, density_hbm, lame_hbm, shear_hbm, gland_hbm, gsea_hbm, gbottom_hbm, bound_hbm,
     inner_high_hbm, inner_low_hbm, across_high_hbm, across_low_hbm,
-    home, coefs, side, edge_high_out, edge_low_out, inner_high_ref, inner_low_ref,
+    *refs,
+):
+    n = len(PIECES)
+    home, refs = refs[:n], refs[n:]
+    (
+    coefs, side, edge_high_out, edge_low_out, inner_high_ref, inner_low_ref,
     xx_ref, zz_ref, xz_ref,
     vx_ref, vz_ref, material_ref, land_ref, density_ref, lame_ref, shear_ref,
     gland_ref, gsea_ref, gbottom_ref, bound_ref, across_high_ref, across_low_ref,
-    packed, outgoing, incoming, returned, load_sem,
-    send_sem, recv_sem, send_back_sem, recv_back_sem,
-):
+    packed,
+    ) = refs[:-5 - 3 * n]
+    outgoing, incoming, returned = refs[-5 - 3 * n:-5 - 2 * n], refs[-5 - 2 * n:-5 - n], refs[-5 - n:-5]
+    load_sem, send_sem, recv_sem, send_back_sem, recv_back_sem = refs[-5:]
     me = lax.axis_index("gx")
-    my_x, my_z = me // RING_Z, me % RING_Z
-
-    def offset(step):
-        group = step // 4
-        half = (group + 1) // 2
-        dz = 4 + half * (1 - 2 * (group % 2))
-        dx = (2 + (step % 4)) % 4
-        return dx, dz
-
-    def ahead(step):
-        dx, dz = offset(step)
-        return ((my_x + dx) % RING_X) * RING_Z + (my_z + dz) % RING_Z
-
-    def behind(step):
-        dx, dz = offset(step)
-        return ((my_x + RING_X - dx) % RING_X) * RING_Z + (my_z + 2 * RING_Z - dz) % RING_Z
-
-    def is_other(step):
-        dx, dz = offset(step)
-        return dx + (dz % RING_Z) != 0
+    my_x, my_z = lax.div(me, RING_Z), lax.rem(me, RING_Z)
+    along_x = [lax.rem(my_x + dx, RING_X) * RING_Z for dx in range(RING_X)]
+    along_z = [lax.rem(my_z + dz, RING_Z) for dz in range(RING_Z)]
+    others = [along_x[dx] + along_z[dz] for dx, dz in ORDER]
 
     barrier = pltpu.get_barrier_semaphore()
-
-    def greet(step, carry):
-        @pl.when(is_other(step))
-        def _():
-            pl.semaphore_signal(barrier, inc=1, device_id={"gx": ahead(step)})
-
-        return carry
-
-    lax.fori_loop(0, OWNERS, greet, 0)
+    for other in others:
+        pl.semaphore_signal(barrier, inc=1, device_id={"gx": other})
 
     pairs = (
         (land_hbm, land_ref), (gland_hbm, gland_ref), (gsea_hbm, gsea_ref),
@@ -234,91 +228,90 @@
 
     packed[0] = jnp.concatenate([stress_xx, stress_xz, part_vx, part_vz], axis=0).T
     packed[1] = jnp.concatenate(
-        [light] + [pltpu.roll(light, NZ - 3 * slot, 1) for slot in range(1, 4)], axis=0
+        [light] + [pltpu.roll(light, NZ - slot, 1) for slot in range(1, 4)], axis=0
     ).T
-    for owner in range(OWNERS):
-        outgoing[owner, :ROWS] = packed[0, ROWS * owner : ROWS * (owner + 1)]
-        outgoing[owner, ROWS:] = packed[1, ROWS * owner : ROWS * owner + CHUNK - ROWS]
-    incoming[me] = outgoing[me]
+    first = 0
+    for piece, rows in enumerate(PIECES):
+        for owner in range(OWNERS):
+            start = ROWS * owner + first
+            outgoing[piece][owner, :rows] = packed[0, start : start + rows]
+            for i in range(rows // 4):
+                outgoing[piece][owner, rows + i : rows + i + 1] = packed[
+                    1, start + 4 * i : start + 4 * i + 1
+                ]
+        incoming[piece][me, : rows + rows // 4] = outgoing[piece][me]
+        first += rows
 
     pl.semaphore_wait(barrier, OWNERS - 1)
 
-    def out_copy(step):
+    def send(source, target, send_semaphore, recv_semaphore):
+        for other in others:
+            pltpu.make_async_remote_copy(
+                src_ref=source.at[other], dst_ref=target.at[me],
+                send_sem=send_semaphore, recv_sem=recv_semaphore, device_id={"gx": other},
+            ).start()
+
+    def all_of(source, target, send_semaphore, recv_semaphore):
         return pltpu.make_async_remote_copy(
-            src_ref=outgoing.at[ahead(step)], dst_ref=incoming.at[me],
-            send_sem=send_sem.at[step], recv_sem=recv_sem.at[step],
-            device_id={"gx": ahead(step)},
+            src_ref=source.at[pl.ds(0, OWNERS - 1)], dst_ref=target.at[pl.ds(0, OWNERS - 1)],
+            send_sem=send_semaphore, recv_sem=recv_semaphore, device_id={"gx": others[0]},
         )
 
-    def in_copy(step):
-        return pltpu.make_async_remote_copy(
-            src_ref=outgoing.at[ahead(step)], dst_ref=incoming.at[behind(step)],
-            send_sem=send_sem.at[step], recv_sem=recv_sem.at[step],
-            device_id={"gx": ahead(step)},
-        )
-
-    def back_copy(step):
-        return pltpu.make_async_remote_copy(
-            src_ref=returned.at[ahead(step)], dst_ref=home.at[me],
-            send_sem=send_back_sem.at[step], recv_sem=recv_back_sem.at[step],
-            device_id={"gx": ahead(step)},
-        )
-
-    def home_copy(step):
-        return pltpu.make_async_remote_copy(
-            src_ref=returned.at[ahead(step)], dst_ref=home.at[behind(step)],
-            send_sem=send_back_sem.at[step], recv_sem=recv_back_sem.at[step],
-            device_id={"gx": ahead(step)},
-        )
-
-    def each_other(act):
-        def step_of(step, carry):
-            @pl.when(is_other(step))
-            def _():
-                act(step)
-
-            return carry
-
-        lax.fori_loop(0, OWNERS, step_of, 0)
-
-    each_other(lambda step: out_copy(step).start())
-    each_other(lambda step: in_copy(step).wait_recv())
+    there, back = [], []
+    for piece, rows in enumerate(PIECES):
+        landing = incoming[piece].at[:, pl.ds(0, rows + rows // 4)]
+        there.append((outgoing[piece], landing, send_sem.at[piece], recv_sem.at[piece]))
+        back.append((returned[piece], home[piece], send_back_sem.at[piece], recv_back_sem.at[piece]))
+        send(*there[piece])
     for load in loads[16:]:
         load.wait()
     across_high, across_low = across_high_ref[...], across_low_ref[...]
 
-    got = incoming[...].reshape(8, 4, CHUNK, LANES)
-    fields = swap_blocks([got[:, k].reshape(8 * CHUNK, LANES) for k in range(4)])
-    row = lax.broadcasted_iota(jnp.int32, (8 * CHUNK, LANES), 0) % CHUNK
-    factor = jnp.zeros((8 * CHUNK, LANES), jnp.float32)
-    for slot in range(4):
-        moved = pltpu.roll(fields[slot], 8 * CHUNK + 3 * slot - ROWS, 0)
-        factor = jnp.where((row >= 3 * slot) & (row < 3 * slot + 3), moved, factor)
-    slope = lateral(fields[:2], across_high, across_low)
-    moved_vx = fields[2] + factor * slope[0]
-    moved_vz = fields[3] + factor * slope[1]
-    slope = lateral([moved_vx, moved_vz], across_high, across_low)
-    back = swap_blocks([moved_vx, moved_vz, slope[0], slope[1]])
-    for k in range(4):
-        for group in range(8):
-            returned[4 * group + k] = back[k][CHUNK * group : CHUNK * group + ROWS]
-    home[me] = returned[me]
-
-    each_other(lambda step: back_copy(step).start())
-    each_other(lambda step: home_copy(step).wait_recv())
-
-    each_other(lambda step: in_copy(step).wait_send())
-    each_other(lambda step: home_copy(step).wait_send())
-
-
-def last_kernel(
-    home, coefs, side, edge_high_ref, edge_low_ref, inner_high_ref, inner_low_ref,
+    for piece, rows in enumerate(PIECES):
+        all_of(*there[piece]).wait_recv()
+        height = 2 * rows
+        got = incoming[piece][...].reshape(8, 4, height, LANES)
+        fields = swap_blocks([got[:, k].reshape(8 * height, LANES) for k in range(4)])
+        row = lax.broadcasted_iota(jnp.int32, (8 * height, LANES), 0) % height
+        factor = jnp.zeros((8 * height, LANES), jnp.float32)
+        for i in range(rows // 4):
+            for slot in range(4):
+                target = 4 * i + slot
+                moved = pltpu.roll(fields[slot], 8 * height + target - (rows + i), 0)
+                factor = jnp.where(row == target, moved, factor)
+        slope = lateral(fields[:2], across_high, across_low)
+        moved_vx = fields[2] + factor * slope[0]
+        moved_vz = fields[3] + factor * slope[1]
+        slope = lateral([moved_vx, moved_vz], across_high, across_low)
+        result = swap_blocks([moved_vx, moved_vz, slope[0], slope[1]])
+        for k in range(4):
+            for group in range(8):
+                returned[piece][4 * group + k] = result[k][height * group : height * group + rows]
+        home[piece][me] = returned[piece][me]
+        send(*back[piece])
+
+    for piece in range(len(PIECES)):
+        all_of(*back[piece]).wait_recv()
+    for piece in range(len(PIECES)):
+        all_of(*there[piece]).wait_send()
+        all_of(*back[piece]).wait_send()
+
+
+def last_kernel(*refs):
+    n = len(PIECES)
+    home, refs = refs[:n], refs[n:]
+    (
+    coefs, side, edge_high_ref, edge_low_ref, inner_high_ref, inner_low_ref,
     xx_ref, zz_ref, xz_ref,
     vx_out, vz_out, xx_out, zz_out, xz_out,
     packed,
-):
-    for owner in range(OWNERS):
-        packed[ROWS * owner : ROWS * (owner + 1)] = home[owner]
+    ) = refs
+    first = 0
+    for piece, rows in enumerate(PIECES):
+        for owner in range(OWNERS):
+            start = ROWS * owner + first
+            packed[start : start + rows] = home[piece][owner]
+        first += rows
     settled = packed[...].T
     next_vx, next_vz = settled[:32], settled[32:64]
     store_lines(vx_out, next_vx)
@@ -368,13 +361,13 @@
     kept = pl.pallas_call(
         kernel,
         out_shape=[
-            pltpu.VMEM((OWNERS, ROWS, LANES), jnp.float32),
+            *[pltpu.VMEM((OWNERS, rows, LANES), jnp.float32) for rows in PIECES],
             pltpu.VMEM((2, 32, NZ), jnp.float32),
             pltpu.VMEM((64, LANES), jnp.int32),
             edge, edge, square, square, lines, lines, lines,
         ],
         in_specs=[hbm] * 18,
-        out_specs=[vmem] * 10,
+        out_specs=[vmem] * (9 + len(PIECES)),
         scratch_shapes=[
             lines, lines,
             pltpu.VMEM((32 * TILES, LANES), jnp.int32),
@@ -384,14 +377,11 @@
             pltpu.VMEM((256, NX), jnp.bfloat16),
             pltpu.VMEM((256, NX), jnp.bfloat16),
             pltpu.VMEM((2, NZ, LANES), jnp.float32),
-            pltpu.VMEM((OWNERS, CHUNK, LANES), jnp.float32),
-            pltpu.VMEM((OWNERS, CHUNK, LANES), jnp.float32),
-            pltpu.VMEM((OWNERS, ROWS, LANES), jnp.float32),
+            *[pltpu.VMEM((OWNERS, rows + rows // 4, LANES), jnp.float32) for rows in PIECES],
+            *[pltpu.VMEM((OWNERS, 2 * rows, LANES), jnp.float32) for rows in PIECES],
+            *[pltpu.VMEM((OWNERS, rows, LANES), jnp.float32) for rows in PIECES],
             pltpu.SemaphoreType.DMA((18,)),
-            pltpu.SemaphoreType.DMA((OWNERS,)),
-            pltpu.SemaphoreType.DMA((OWNERS,)),
-            pltpu.SemaphoreType.DMA((OWNERS,)),
-            pltpu.SemaphoreType.DMA((OWNERS,)),
+            *[pltpu.SemaphoreType.DMA((len(PIECES),))] * 4,
         ],
         compiler_params=pltpu.CompilerParams(
             collective_id=0, has_side_effects=True, vmem_limit_bytes=VMEM_KIB * 1024
@@ -405,7 +395,7 @@
     outs = pl.pallas_call(
         last_kernel,
         out_shape=[jax.ShapeDtypeStruct((32 * TILES, LANES), jnp.float32)] * 5,
-        in_specs=[vmem] * 10,
+        in_specs=[vmem] * (9 + len(PIECES)),
         out_specs=[vmem] * 5,
         scratch_shapes=[pltpu.VMEM((NZ, LANES), jnp.float32)],
         compiler_params=pltpu.CompilerParams(vmem_limit_bytes=8 * 2**20),

time: 31.2 us -> 27.3 us (0.88)
  Pallas kernels: 30.4 us -> 26.5 us
    pallas_call x1, Pallas kernels: 29.4 us -> 25.5 us  [body(): pl.pallas_call(kernel, out_shape=[*[pltpu.VMEM((OWNERS, rows, LANES), jnp...]
where the time goes in v2:
time: 27.3 us; the launch traced here: 27.2 us
  Pallas kernels  26.5 us (97%)
  between operations  0.64 us (2%)
    pallas_call x1, Pallas kernels, body(): pl.pallas_call(kernel, out_shape=[*[pltpu.VMEM((OWNERS, rows, LANES), jnp...  25.5 us
    pallas_call x1, Pallas kernels, body(): pl.pallas_call(last_kernel, out_shape=[jax.ShapeDtypeStruct((32 * TILES,...  1.05 us

profile of v2, /device:TPU:8, one launch (start us, length us, event | category | flops | bytes accessed | tf_op | source)
XLA Modules:
  0.0 27.2 jit_solution(6611256423266189954)
XLA Ops:
  0.6 25.5 %shard_map.209 = (f32[32,4,128]{2,1,0:T(4,128)S(1)}, f32[32,8,128]{2,1,0:T(8,128)S(1)}, f32[2,32,384]{2,1,0:T(8,128)S(1)}, s32[64,128]{1,0:T(8,128)S(1)}, bf16[1...) custom-call(f32[96,128]{1,0:T(8,128)} %bitcast.12, ...), custom_call_target="tpu_custom_call" | custom-call | tf_op jit(solution)/shard_map/pallas_call | solution.py:361
  26.1 1.1 %shard_map.210 = (f32[96,128]{1,0:T(8,128)}, f32[96,128]{1,0:T(8,128)}, f32[96,128]{1,0:T(8,128)}, f32[96,128]{1,0:T(8,128)}, f32[96,128]{1,0:T(8,128)}) custom-call(f32[32,4,128]{2,1,0:T(4,128)S(1)} %get-tuple-element.21.refs_0_, f32[32,8,128]{2,1,0:T(8,128)S(1)} %get-tuple-element.22.refs_1_, f32[2,32,384]{2,1,0:T(8,128)S(1)} %get-tuple-element.23.refs_2_, ...), custom_call_target="tpu_custom_call" | custom-call | tf_op jit(solution)/shard_map/pallas_call | solution.py:395

commit v3 on v2

--- a/solution.py
+++ b/solution.py
@@ -16,22 +16,27 @@
 RING_X = 4
 RING_Z = 8
 OWNERS = 32
-ROWS = 12
-CHUNK = 16
+HALF = RING_Z // 2
+LATE_X = 2
+HOLDERS = RING_X * HALF + LATE_X * HALF
+ROWS = NZ // HOLDERS
 LANES = 128
 TILES = 3
 TIME_STEP = 0.2
 VMEM_KIB = 63900
-
-
-ORDER = [
-    (dx, sign * dz % RING_Z)
-    for dz in (4, 3, 2, 1, 0)
-    for dx in (2, 1, 3, 0)
-    for sign in ((1, -1) if dz % 4 else (1,))
-    if dx or dz
-]
-PIECES = (4, 8)
+PIECES = (4, 4, 8)
+
+
+def chunk_rows(rows):
+    return rows + rows // 4
+
+
+def height_of(rows):
+    return -(-chunk_rows(rows) // 8) * 8
+
+
+def block_of(rows):
+    return max(rows, 8)
 
 
 def spectral(length):
@@ -145,13 +150,40 @@
     load_sem, send_sem, recv_sem, send_back_sem, recv_back_sem = refs[-5:]
     me = lax.axis_index("gx")
     my_x, my_z = lax.div(me, RING_Z), lax.rem(me, RING_Z)
-    along_x = [lax.rem(my_x + dx, RING_X) * RING_Z for dx in range(RING_X)]
-    along_z = [lax.rem(my_z + dz, RING_Z) for dz in range(RING_Z)]
-    others = [along_x[dx] + along_z[dz] for dx, dz in ORDER]
+    early = my_z < HALF
+    holding = early | (my_x < LATE_X)
+    my_slot = jnp.where(early, my_x * HALF + my_z, RING_X * HALF + my_x * HALF + my_z - HALF)
+    any_x = [lax.rem(my_x + dx, RING_X) for dx in range(RING_X)]
+    late_x = [lax.rem(my_x + dx, LATE_X) for dx in range(LATE_X)]
+    half_z = [lax.rem(my_z + dz, HALF) for dz in range(HALF)]
+
+    def group(columns, first_z, first_slot, far):
+        found = []
+        for x in columns[::-1] if far else columns:
+            for z in half_z[::-1] if far else half_z:
+                found.append((x * RING_Z + first_z + z, first_slot + x * HALF + z))
+        return found
+
+    early_ones = group(any_x, 0, 0, True)
+    late_holders = group(late_x, HALF, RING_X * HALF, True)
+    late_ones = group(any_x, HALF, 0, True)
+
+    def each_other(members, act):
+        for index, (device, slot) in enumerate(members):
+            if index < len(members) - 1:
+                act(device, slot)
+            else:
+                pl.when(device != me)(functools.partial(act, device, slot))
 
     barrier = pltpu.get_barrier_semaphore()
-    for other in others:
-        pl.semaphore_signal(barrier, inc=1, device_id={"gx": other})
+
+    def greet(device, slot):
+        pl.semaphore_signal(barrier, inc=1, device_id={"gx": device})
+
+    @pl.when(holding)
+    def _():
+        each_other(early_ones, greet)
+        each_other(late_ones, greet)
 
     pairs = (
         (land_hbm, land_ref), (gland_hbm, gland_ref), (gsea_hbm, gsea_ref),
@@ -232,44 +264,52 @@
     ).T
     first = 0
     for piece, rows in enumerate(PIECES):
-        for owner in range(OWNERS):
-            start = ROWS * owner + first
-            outgoing[piece][owner, :rows] = packed[0, start : start + rows]
+        for holder in range(HOLDERS):
+            start = ROWS * holder + first
+            outgoing[piece][holder, :rows] = packed[0, start : start + rows]
             for i in range(rows // 4):
-                outgoing[piece][owner, rows + i : rows + i + 1] = packed[
+                outgoing[piece][holder, rows + i : rows + i + 1] = packed[
                     1, start + 4 * i : start + 4 * i + 1
                 ]
-        incoming[piece][me, : rows + rows // 4] = outgoing[piece][me]
         first += rows
 
-    pl.semaphore_wait(barrier, OWNERS - 1)
-
-    def send(source, target, send_semaphore, recv_semaphore):
-        for other in others:
+    @pl.when(holding)
+    def _():
+        for piece, rows in enumerate(PIECES):
+            incoming[piece][me, : chunk_rows(rows)] = outgoing[piece][my_slot]
+        pl.semaphore_wait(barrier, HOLDERS - 1)
+
+    @pl.when(jnp.logical_not(holding))
+    def _():
+        pl.semaphore_wait(barrier, HOLDERS)
+
+    def bulk(ref, count, send_semaphore, recv_semaphore):
+        return pltpu.make_async_remote_copy(
+            src_ref=ref.at[pl.ds(0, count)], dst_ref=ref.at[pl.ds(0, count)],
+            send_sem=send_semaphore, recv_sem=recv_semaphore, device_id={"gx": early_ones[0][0]},
+        )
+
+    landings = [
+        incoming[piece].at[:, pl.ds(0, chunk_rows(rows))] for piece, rows in enumerate(PIECES)
+    ]
+    for piece in range(len(PIECES)):
+
+        def send(device, slot, piece=piece):
             pltpu.make_async_remote_copy(
-                src_ref=source.at[other], dst_ref=target.at[me],
-                send_sem=send_semaphore, recv_sem=recv_semaphore, device_id={"gx": other},
+                src_ref=outgoing[piece].at[slot], dst_ref=landings[piece].at[me],
+                send_sem=send_sem.at[piece], recv_sem=recv_sem.at[piece],
+                device_id={"gx": device},
             ).start()
 
-    def all_of(source, target, send_semaphore, recv_semaphore):
-        return pltpu.make_async_remote_copy(
-            src_ref=source.at[pl.ds(0, OWNERS - 1)], dst_ref=target.at[pl.ds(0, OWNERS - 1)],
-            send_sem=send_semaphore, recv_sem=recv_semaphore, device_id={"gx": others[0]},
-        )
-
-    there, back = [], []
-    for piece, rows in enumerate(PIECES):
-        landing = incoming[piece].at[:, pl.ds(0, rows + rows // 4)]
-        there.append((outgoing[piece], landing, send_sem.at[piece], recv_sem.at[piece]))
-        back.append((returned[piece], home[piece], send_back_sem.at[piece], recv_back_sem.at[piece]))
-        send(*there[piece])
+        each_other(late_holders, send)
+        each_other(early_ones, send)
     for load in loads[16:]:
         load.wait()
-    across_high, across_low = across_high_ref[...], across_low_ref[...]
-
-    for piece, rows in enumerate(PIECES):
-        all_of(*there[piece]).wait_recv()
-        height = 2 * rows
+
+    def hold(piece, rows):
+        across_high, across_low = across_high_ref[...], across_low_ref[...]
+        bulk(landings[piece], OWNERS - 1, send_sem.at[piece], recv_sem.at[piece]).wait_recv()
+        height, block = height_of(rows), block_of(rows)
         got = incoming[piece][...].reshape(8, 4, height, LANES)
         fields = swap_blocks([got[:, k].reshape(8 * height, LANES) for k in range(4)])
         row = lax.broadcasted_iota(jnp.int32, (8 * height, LANES), 0) % height
@@ -279,22 +319,50 @@
                 target = 4 * i + slot
                 moved = pltpu.roll(fields[slot], 8 * height + target - (rows + i), 0)
                 factor = jnp.where(row == target, moved, factor)
+        fields, factor = [
+            [f.reshape(8, height, LANES)[:, :block].reshape(8 * block, LANES) for f in part]
+            for part in (fields, [factor])
+        ]
         slope = lateral(fields[:2], across_high, across_low)
-        moved_vx = fields[2] + factor * slope[0]
-        moved_vz = fields[3] + factor * slope[1]
+        moved_vx = fields[2] + factor[0] * slope[0]
+        moved_vz = fields[3] + factor[0] * slope[1]
         slope = lateral([moved_vx, moved_vz], across_high, across_low)
         result = swap_blocks([moved_vx, moved_vz, slope[0], slope[1]])
         for k in range(4):
-            for group in range(8):
-                returned[piece][4 * group + k] = result[k][height * group : height * group + rows]
-        home[piece][me] = returned[piece][me]
-        send(*back[piece])
-
-    for piece in range(len(PIECES)):
-        all_of(*back[piece]).wait_recv()
-    for piece in range(len(PIECES)):
-        all_of(*there[piece]).wait_send()
-        all_of(*back[piece]).wait_send()
+            for part in range(8):
+                returned[piece][4 * part + k] = result[k][block * part : block * part + rows]
+        home[piece][my_slot] = returned[piece][me]
+
+        def send(device, slot):
+            pltpu.make_async_remote_copy(
+                src_ref=returned[piece].at[device], dst_ref=home[piece].at[my_slot],
+                send_sem=send_back_sem.at[piece], recv_sem=recv_back_sem.at[piece],
+                device_id={"gx": device},
+            ).start()
+
+        each_other(early_ones, send)
+        each_other(late_ones, send)
+
+    @pl.when(holding)
+    def _():
+        for piece, rows in enumerate(PIECES):
+            hold(piece, rows)
+
+    def settle(count):
+        for piece in range(len(PIECES)):
+            bulk(home[piece], count, send_back_sem.at[piece], recv_back_sem.at[piece]).wait_recv()
+        for piece in range(len(PIECES)):
+            bulk(outgoing[piece], count, send_sem.at[piece], recv_sem.at[piece]).wait_send()
+
+    @pl.when(holding)
+    def _():
+        settle(HOLDERS - 1)
+        for piece in range(len(PIECES)):
+            bulk(returned[piece], OWNERS - 1, send_back_sem.at[piece], recv_back_sem.at[piece]).wait_send()
+
+    @pl.when(jnp.logical_not(holding))
+    def _():
+        settle(HOLDERS)
 
 
 def last_kernel(*refs):
@@ -308,9 +376,9 @@
     ) = refs
     first = 0
     for piece, rows in enumerate(PIECES):
-        for owner in range(OWNERS):
-            start = ROWS * owner + first
-            packed[start : start + rows] = home[piece][owner]
+        for holder in range(HOLDERS):
+            start = ROWS * holder + first
+            packed[start : start + rows] = home[piece][holder]
         first += rows
     settled = packed[...].T
     next_vx, next_vz = settled[:32], settled[32:64]
@@ -361,7 +429,7 @@
     kept = pl.pallas_call(
         kernel,
         out_shape=[
-            *[pltpu.VMEM((OWNERS, rows, LANES), jnp.float32) for rows in PIECES],
+            *[pltpu.VMEM((HOLDERS, rows, LANES), jnp.float32) for rows in PIECES],
             pltpu.VMEM((2, 32, NZ), jnp.float32),
             pltpu.VMEM((64, LANES), jnp.int32),
             edge, edge, square, square, lines, lines, lines,
@@ -377,8 +445,8 @@
             pltpu.VMEM((256, NX), jnp.bfloat16),
             pltpu.VMEM((256, NX), jnp.bfloat16),
             pltpu.VMEM((2, NZ, LANES), jnp.float32),
-            *[pltpu.VMEM((OWNERS, rows + rows // 4, LANES), jnp.float32) for rows in PIECES],
-            *[pltpu.VMEM((OWNERS, 2 * rows, LANES), jnp.float32) for rows in PIECES],
+            *[pltpu.VMEM((HOLDERS, chunk_rows(rows), LANES), jnp.float32) for rows in PIECES],
+            *[pltpu.VMEM((OWNERS, height_of(rows), LANES), jnp.float32) for rows in PIECES],
             *[pltpu.VMEM((OWNERS, rows, LANES), jnp.float32) for rows in PIECES],
             pltpu.SemaphoreType.DMA((18,)),
             *[pltpu.SemaphoreType.DMA((len(PIECES),))] * 4,

time: 27.3 us -> 26.9 us (0.985)
  Pallas kernels: 26.5 us -> 26.2 us
    pallas_call x1, Pallas kernels: 25.5 us -> 25.1 us  [body(): pl.pallas_call(kernel, out_shape=[*[pltpu.VMEM((HOLDERS, rows, LANES), jn...]
where the time goes in v3:
time: 26.9 us; the launch traced here: 26.8 us
  Pallas kernels  26.2 us (97%)
  between operations  0.64 us (2%)
    pallas_call x1, Pallas kernels, body(): pl.pallas_call(kernel, out_shape=[*[pltpu.VMEM((HOLDERS, rows, LANES), jn...  25.1 us
    pallas_call x1, Pallas kernels, body(): pl.pallas_call(last_kernel, out_shape=[jax.ShapeDtypeStruct((32 * TILES,...  1.06 us

profile of v3, /device:TPU:8, one launch (start us, length us, event | category | flops | bytes accessed | tf_op | source)
XLA Modules:
  0.0 26.8 jit_solution(2787125754983170046)
XLA Ops:
  0.6 25.1 %shard_map.209 = (f32[24,4,128]{2,1,0:T(4,128)S(1)}, f32[24,4,128]{2,1,0:T(4,128)S(1)}, f32[24,8,128]{2,1,0:T(8,128)S(1)}, f32[2,32,384]{2,1,0:T(8,128)S(1)}, s3...) custom-call(f32[96,128]{1,0:T(8,128)} %bitcast.12, ...), custom_call_target="tpu_custom_call" | custom-call | tf_op jit(solution)/shard_map/pallas_call | solution.py:429
  25.8 1.1 %shard_map.210 = (f32[96,128]{1,0:T(8,128)}, f32[96,128]{1,0:T(8,128)}, f32[96,128]{1,0:T(8,128)}, f32[96,128]{1,0:T(8,128)}, f32[96,128]{1,0:T(8,128)}) custom-call(f32[24,4,128]{2,1,0:T(4,128)S(1)} %get-tuple-element.22.refs_0_, f32[24,4,128]{2,1,0:T(4,128)S(1)} %get-tuple-element.23.refs_1_, f32[24,8,128]{2,1,0:T(8,128)S(1)} %get-tuple-element.24.refs_2_, ...), custom_call_target="tpu_custom_call" | custom-call | tf_op jit(solution)/shard_map/pallas_call | solution.py:463

commit v4 on v3

--- a/solution.py
+++ b/solution.py
@@ -259,18 +259,17 @@
     part_vz = load_lines(vz_ref) + light * depth[32:]
 
     packed[0] = jnp.concatenate([stress_xx, stress_xz, part_vx, part_vz], axis=0).T
-    packed[1] = jnp.concatenate(
-        [light] + [pltpu.roll(light, NZ - slot, 1) for slot in range(1, 4)], axis=0
-    ).T
+    for quarter in (1, 2):
+        packed[quarter] = jnp.concatenate(
+            [light] + [pltpu.roll(light, NZ - quarter * slot, 1) for slot in range(1, 4)], axis=0
+        ).T
     first = 0
     for piece, rows in enumerate(PIECES):
         for holder in range(HOLDERS):
             start = ROWS * holder + first
             outgoing[piece][holder, :rows] = packed[0, start : start + rows]
-            for i in range(rows // 4):
-                outgoing[piece][holder, rows + i : rows + i + 1] = packed[
-                    1, start + 4 * i : start + 4 * i + 1
-                ]
+            quarter = rows // 4
+            outgoing[piece][holder, rows:] = packed[quarter, start : start + quarter]
         first += rows
 
     @pl.when(holding)
@@ -292,40 +291,52 @@
     landings = [
         incoming[piece].at[:, pl.ds(0, chunk_rows(rows))] for piece, rows in enumerate(PIECES)
     ]
-    for piece in range(len(PIECES)):
-
-        def send(device, slot, piece=piece):
-            pltpu.make_async_remote_copy(
-                src_ref=outgoing[piece].at[slot], dst_ref=landings[piece].at[me],
-                send_sem=send_sem.at[piece], recv_sem=recv_sem.at[piece],
-                device_id={"gx": device},
-            ).start()
-
-        each_other(late_holders, send)
-        each_other(early_ones, send)
+    def send(piece, device, slot):
+        pltpu.make_async_remote_copy(
+            src_ref=outgoing[piece].at[slot], dst_ref=landings[piece].at[me],
+            send_sem=send_sem.at[piece], recv_sem=recv_sem.at[piece], device_id={"gx": device},
+        ).start()
+
+    def send_to(members, *pieces):
+        for piece in pieces:
+            each_other(members, functools.partial(send, piece))
+
+    every = range(len(PIECES))
+
+    @pl.when(early)
+    def _():
+        for piece in every:
+            send_to(late_holders, piece)
+            send_to(early_ones, piece)
+
+    @pl.when(jnp.logical_not(early))
+    def _():
+        for piece in every:
+            send_to(early_ones, piece)
+            send_to(late_holders, piece)
+
     for load in loads[16:]:
         load.wait()
 
     def hold(piece, rows):
         across_high, across_low = across_high_ref[...], across_low_ref[...]
         bulk(landings[piece], OWNERS - 1, send_sem.at[piece], recv_sem.at[piece]).wait_recv()
-        height, block = height_of(rows), block_of(rows)
+        height, block, quarter = height_of(rows), block_of(rows), rows // 4
         got = incoming[piece][...].reshape(8, 4, height, LANES)
-        fields = swap_blocks([got[:, k].reshape(8 * height, LANES) for k in range(4)])
-        row = lax.broadcasted_iota(jnp.int32, (8 * height, LANES), 0) % height
-        factor = jnp.zeros((8 * height, LANES), jnp.float32)
-        for i in range(rows // 4):
-            for slot in range(4):
-                target = 4 * i + slot
-                moved = pltpu.roll(fields[slot], 8 * height + target - (rows + i), 0)
-                factor = jnp.where(row == target, moved, factor)
-        fields, factor = [
-            [f.reshape(8, height, LANES)[:, :block].reshape(8 * block, LANES) for f in part]
-            for part in (fields, [factor])
+        tiles = [
+            swap_blocks([got[:, k, a : a + 8].reshape(8 * 8, LANES) for k in range(4)])
+            for a in range(0, height, 8)
         ]
+        fields, lights = tiles[0], tiles[-1]
+        row = lax.broadcasted_iota(jnp.int32, (8 * 8, LANES), 0) % 8
+        factor = jnp.zeros((8 * 8, LANES), jnp.float32)
+        for slot in range(4):
+            moved = pltpu.roll(lights[slot], (64 + quarter * slot - rows % 8) % 64, 0)
+            own = (row >= quarter * slot) & (row < quarter * (slot + 1))
+            factor = jnp.where(own, moved, factor)
         slope = lateral(fields[:2], across_high, across_low)
-        moved_vx = fields[2] + factor[0] * slope[0]
-        moved_vz = fields[3] + factor[0] * slope[1]
+        moved_vx = fields[2] + factor * slope[0]
+        moved_vz = fields[3] + factor * slope[1]
         slope = lateral([moved_vx, moved_vz], across_high, across_low)
         result = swap_blocks([moved_vx, moved_vz, slope[0], slope[1]])
         for k in range(4):
@@ -444,7 +455,7 @@
             pltpu.VMEM((CONT, NZ), jnp.float32),
             pltpu.VMEM((256, NX), jnp.bfloat16),
             pltpu.VMEM((256, NX), jnp.bfloat16),
-            pltpu.VMEM((2, NZ, LANES), jnp.float32),
+            pltpu.VMEM((3, NZ, LANES), jnp.float32),
             *[pltpu.VMEM((HOLDERS, chunk_rows(rows), LANES), jnp.float32) for rows in PIECES],
             *[pltpu.VMEM((OWNERS, height_of(rows), LANES), jnp.float32) for rows in PIECES],
             *[pltpu.VMEM((OWNERS, rows, LANES), jnp.float32) for rows in PIECES],

time: 26.9 us -> 26.8 us (level)
  Pallas kernels: 26.2 us -> 25.9 us
    pallas_call x1, Pallas kernels: 25.1 us -> 24.8 us  [body(): pl.pallas_call(kernel, out_shape=[*[pltpu.VMEM((HOLDERS, rows, LANES), jn...]
where the time goes in v4:
time: 26.8 us; the launch traced here: 26.5 us
  Pallas kernels  25.9 us (97%)
  between operations  0.64 us (2%)
    pallas_call x1, Pallas kernels, body(): pl.pallas_call(kernel, out_shape=[*[pltpu.VMEM((HOLDERS, rows, LANES), jn...  24.8 us
    pallas_call x1, Pallas kernels, body(): pl.pallas_call(last_kernel, out_shape=[jax.ShapeDtypeStruct((32 * TILES,...  1.05 us

profile of v4, /device:TPU:8, one launch (start us, length us, event | category | flops | bytes accessed | tf_op | source)
XLA Modules:
  0.0 26.5 jit_solution(15265129877171296254)
XLA Ops:
  0.6 24.8 %shard_map.209 = (f32[24,4,128]{2,1,0:T(4,128)S(1)}, f32[24,4,128]{2,1,0:T(4,128)S(1)}, f32[24,8,128]{2,1,0:T(8,128)S(1)}, f32[2,32,384]{2,1,0:T(8,128)S(1)}, s3...) custom-call(f32[96,128]{1,0:T(8,128)} %bitcast.12, ...), custom_call_target="tpu_custom_call" | custom-call | tf_op jit(solution)/shard_map/pallas_call | solution.py:440
  25.5 1.1 %shard_map.210 = (f32[96,128]{1,0:T(8,128)}, f32[96,128]{1,0:T(8,128)}, f32[96,128]{1,0:T(8,128)}, f32[96,128]{1,0:T(8,128)}, f32[96,128]{1,0:T(8,128)}) custom-call(f32[24,4,128]{2,1,0:T(4,128)S(1)} %get-tuple-element.22.refs_0_, f32[24,4,128]{2,1,0:T(4,128)S(1)} %get-tuple-element.23.refs_1_, f32[24,8,128]{2,1,0:T(8,128)S(1)} %get-tuple-element.24.refs_2_, ...), custom_call_target="tpu_custom_call" | custom-call | tf_op jit(solution)/shard_map/pallas_call | solution.py:474
